TPU v7x, 32 devices: a 4x4x1 block of a 4x4x8 slice. The times are simulated.
32 devices in a mesh: batch: 1 (over z), row: 4 (over y), col: 8 (over x, core).
Axes of the slice: x: 4, y: 4, z: 1, core: 2. Of those that a mesh axis runs over, the one named last changes fastest.
The devices are a block of a 4x4x8 slice.
Arguments:
- l_mat: bfloat16 [8192, 8192], P(('batch', 'row'), 'col')
- b_mat: bfloat16 [8192, 16384], P(('batch', 'row'), 'col')
Outputs:
- output: bfloat16 [8192, 16384], P(('batch', 'row'), 'col')
All inputs are finite; a program needn't handle non-finite values.
Results may differ from a plain program's by a relative error of at most 0.001.
Values are sent between devices in bfloat16 or wider.
A program may use at most 768 MiB of HBM per device.

v0:
```python
import functools

import jax
import jax.numpy as jnp
from jax import lax
from jax.experimental import pallas as pl
from jax.experimental.pallas import tpu as pltpu
from jax.sharding import PartitionSpec as P

MESH = pl.DeviceIdType.MESH
CHUNKS = 4
TILES = 8
SLOTS = 2

ORDERS = (
    "00 01 10 11 02 12 03 13 04 14 20 21 22 23 24 05 15 25 06 16 26 30 31 32 33 34 35 36 07 17 27 37",
    "00 01 10 11 02 12 03 13 20 21 22 23 04 14 24 05 15 25 30 31 32 33 34 35 06 16 26 36 07 17 27 37",
    "00 01 02 03 10 11 12 13 20 21 22 23 04 14 24 30 31 32 33 34 05 15 25 35 06 16 26 36 07 17 27 37",
)
FORWARD_AT = (0, 0, 3, 5, 8, 14, 18, 23)
EXTRA, LOAD_B, FRESH_B, LOAD_L = 32, 64, 128, 256


def codes(order):
    tiles = [(0, int(t[0]), int(t[1])) for t in order.split()]
    tiles += [(1, i, j) for i in range(CHUNKS) for j in range(TILES)]
    out = []
    for n, (extra, i, j) in enumerate(tiles):
        code = i * TILES + j + EXTRA * extra
        if n == 0 or tiles[n - 1][2] != j or tiles[n - 1][0] != extra:
            code += LOAD_B
        if (extra, j) not in [(e, b) for e, _, b in tiles[:n]]:
            code += FRESH_B
        if (extra, i) not in [(e, a) for e, a, _ in tiles[:n]]:
            code += LOAD_L
        out.append(code)
    return out


def kernel(nrow, nx, l_ref, b_ref, x_ref, bg, lb, lv, bv, ov, acc,
           br, bs, bs2, gr, wr, ls, ps, ly, inj, lvs, bvs, xs, xr):
    rows, width = l_ref.shape
    cols = b_ref.shape[1]
    rc, half, tw = rows // CHUNKS, rows // CHUNKS // 2, cols // TILES

    row, col = lax.axis_index("row"), lax.axis_index("col")
    x, core = col // 2, col % 2
    right, left = (x + 1) % nx, (x + nx - 1) % nx
    up, down = (row + nrow - 1) % nrow, (row + 1) % nrow
    low = row < 2
    mirror = nrow - 1 - row
    wcore = jnp.where(low, 1, 0)
    gcore = 1 - wcore
    pmain = jnp.where(low, mirror, row)
    is_w, is_g = core == wcore, core == gcore
    low_w, low_g = jnp.logical_and(low, is_w), jnp.logical_and(low, is_g)
    high_w, high_g = jnp.logical_and(~low, is_w), jnp.logical_and(~low, is_g)

    def both(*conditions):
        return functools.reduce(jnp.logical_and, conditions)

    def needed(p, c, i):
        return jnp.logical_or(c <= 2 * p, jnp.logical_and(c == 2 * p + 1, i >= CHUNKS // 2))

    def device(r, xx, k):
        return {"row": r, "col": xx * 2 + k}

    partner = device(row, x, 1 - core)

    def remote(src, dst, send, recv, to):
        return pltpu.make_async_remote_copy(
            src_ref=src, dst_ref=dst, send_sem=send, recv_sem=recv, device_id=to, device_id_type=MESH)

    def arrived(ref, sem):
        pltpu.make_async_copy(ref, ref, sem).wait()

    def sent(ref, sem):
        pltpu.make_async_copy(ref, ref, sem).wait()

    def each(n, body):
        lax.fori_loop(0, n, lambda k, carry: (body(k), carry)[1], 0)

    barrier = pltpu.get_barrier_semaphore()
    peers = [partner] + [device(r, xx, k) for k in (0, 1)
                         for r, xx in ((row, right), (row, left), (up, x), (down, x))]
    for peer in peers:
        pl.semaphore_signal(barrier, inc=1, device_id=peer, device_id_type=MESH)
    pl.semaphore_wait(barrier, len(peers))

    def lrows(i):
        return pl.ds(pl.multiple_of(i * rc, rc), rc)

    def lhalf(i, d):
        return pl.ds(pl.multiple_of(i * rc + d * half, half), half)

    def bcols(j):
        return pl.ds(pl.multiple_of(j * tw, tw), tw)

    def gpiece(m, c, i, d):
        return lb.at[m, c, lhalf(i, d), :]

    def wpiece(m, c, i):
        return lb.at[m, c, lrows(i), :]

    def l_to_mirror(i):
        return remote(l_ref.at[lrows(i), :], wpiece(0, col, i), ly.at[i], gr.at[0, i, col, 0], device(mirror, x, 0))

    def l_own(m, i, d):
        return remote(l_ref.at[lhalf(i, d), :], gpiece(m, col, i, d), ls.at[m, i, col, d], gr.at[m, i, col, d],
                      device(row, right if d == 0 else left, gcore))

    def l_to_partner(m, i):
        return remote(l_ref.at[lrows(i), :], wpiece(m, col, i), ly.at[i], gr.at[m, i, col, 0], partner)

    first_row = jnp.where(core == 0,
                          jnp.where(row == 1, 2, 3),
                          jnp.where(row == 1, 0, jnp.where(row == 3, 0, 1)))

    def b_first(j):
        return remote(b_ref.at[:, bcols(j)], bg.at[row, :, bcols(j)], bs.at[j], br.at[row, j], device(first_row, x, core))

    def b_again(j):
        return remote(b_ref.at[:, bcols(j)], bg.at[0, :, bcols(j)], bs2.at[j], br.at[0, j], device(1, x, 0))

    fq = jnp.where(row == 3, 0, jnp.where(row == 2, 1, 2))
    ft = jnp.where(row == 3, 2, jnp.where(row == 2, 3, 0))
    forwards = jnp.logical_and(is_w, row > 0)

    def b_forward(j):
        ref = bg.at[fq, :, bcols(j)]
        return remote(ref, ref, bs2.at[j], br.at[fq, j], device(ft, x, core))

    def forward(j):
        arrived(bg.at[fq, :, bcols(j)], br.at[fq, j])
        b_forward(j).start()

    sends_b = ~both(row == 3, core == 0)
    g0 = both(row == 0, core == 0)
    w2 = both(row == 2, core == 0)

    def start_b(*js):
        for j in js:
            b_first(j).start()

    def start_l(i):
        @pl.when(needed(row, col, i))
        def _():
            l_to_mirror(i).start()

    @pl.when(is_w)
    def _():
        def go(i):
            @pl.when(needed(row, col, i))
            def _():
                m = jnp.where(low, 1, 0)
                l_own(m, i, 0).start()
                l_own(m, i, 1).start()

                @pl.when(low)
                def _():
                    l_to_partner(1, i).start()
        each(CHUNKS, go)

    @pl.when(high_w)
    def _():
        each(CHUNKS, start_l)

        def go(j):
            @pl.when(w2)
            def _():
                b_first(j).start()
            forward(j)
        each(TILES, go)

    @pl.when(both(high_g, row == 3))
    def _():
        start_l(0)
        start_l(1)
        start_b(0)
        start_l(2)
        start_b(1)
        start_l(3)
        start_b(*range(2, TILES))

    @pl.when(both(high_g, row == 2))
    def _():
        each(CHUNKS, start_l)
        each(TILES, lambda j: b_first(j).start())

    @pl.when(low)
    def _():
        each(TILES, lambda j: b_first(j).start())

    def product(a, k0, i, slot, p, t, deep):
        def dot(first, depth):
            lhs = lv[a, :, pl.ds(pl.multiple_of(k0 + first, rows), depth)]
            return jnp.dot(lhs, bv[slot, pl.ds(first, depth), :], preferred_element_type=jnp.float32)

        if deep:
            @pl.when(p >= 2)
            def _():
                acc[...] = dot(0, 2 * rows)
        for odd in (0, 1):
            for chunk in range(CHUNKS):
                depth = odd * rows + (chunk + 1) * rc

                @pl.when(both(p % 2 == odd, i == chunk))
                def _():
                    if deep:
                        last = dot(pl.multiple_of(p // 2 * (2 * rows), rows), depth)
                        ov[t] = (jnp.where(p >= 2, acc[...], 0.0) + last).astype(ov.dtype)
                    else:
                        ov[t] = dot(0, depth).astype(ov.dtype)

    def place(m, i):
        return jnp.where(m == 0, i, CHUNKS), jnp.where(m == 0, 0, i % 2 * (2 * rows))

    def copy_l(m, i, c, local):
        a, k0 = place(m, i)
        src = l_ref.at[lrows(i), :] if local else wpiece(m, c, i)
        to = lv.at[a, :, pl.ds(pl.multiple_of(k0 + c * width, width), width)]
        return pltpu.make_async_copy(src, to, lvs.at[c])

    def load_l(m, p, i, own, wait):
        def start(c):
            @pl.when(needed(p, c, i))
            def _():
                mine = jnp.logical_and(own, c == col)

                @pl.when(mine)
                def _():
                    copy_l(m, i, c, True).start()

                @pl.when(~mine)
                def _():
                    if wait:
                        arrived(wpiece(m, c, i), wr.at[m, i, c])
                    copy_l(m, i, c, False).start()
        each(2 * nx, start)

    def loaded_l(m, p, i):
        def finish(c):
            @pl.when(needed(p, c, i))
            def _():
                copy_l(m, i, c, True).wait()
        each(2 * nx, finish)

    def load_b(q, j, slot):
        def copy(local):
            src = b_ref.at[:, bcols(j)] if local else bg.at[q, :, bcols(j)]
            to = bv.at[slot, pl.ds(q * rows, rows), :]
            return pltpu.make_async_copy(src, to, bvs.at[slot, q])

        @pl.when(q == row)
        def _():
            copy(True).start()

        @pl.when(q != row)
        def _():
            copy(False).start()

    def loaded_b(q, slot):
        pltpu.make_async_copy(b_ref.at[:, bcols(0)], bv.at[slot, pl.ds(q * rows, rows), :], bvs.at[slot, q]).wait()

    def x_home(t, i, j):
        return remote(ov.at[t], x_ref.at[lrows(i), bcols(j)], xs.at[t], xr, device(mirror, x, core))

    def x_here(t, i, j):
        return pltpu.make_async_copy(ov.at[t], x_ref.at[lrows(i), bcols(j)], xs.at[t])

    def extra_rows(i):
        a, k0 = place(1, i)

        def start(j):
            for q in (0, 1):
                @pl.when(q <= row)
                def _():
                    @pl.when(jnp.logical_and(q != row, i == 0))
                    def _():
                        arrived(bg.at[q, :, bcols(j)], br.at[q, j])
                    load_b(q, j, j % SLOTS)

        load_l(1, row, i, True, False)
        start(0)
        loaded_l(1, row, i)

        def tile(j):
            for q in (0, 1):
                @pl.when(q <= row)
                def _():
                    loaded_b(q, j % SLOTS)

            @pl.when(j < TILES - 1)
            def _():
                start(j + 1)
            product(a, k0, i, j % SLOTS, row, i * TILES + j, False)
            x_here(i * TILES + j, i, j).start()
        each(TILES, tile)

    def hand(m, c, i, d):
        ref = gpiece(m, c, i, d)
        return remote(ref, ref, ps.at[m, i, c, d], wr.at[m, i, c], partner)

    def hand_own(m, i, d):
        return remote(l_ref.at[lhalf(i, d), :], gpiece(m, col, i, d), ps.at[m, i, col, d], wr.at[m, i, col], partner)

    def pass_on(m, c, i, d):
        ref = gpiece(m, c, i, d)
        return remote(ref, ref, ls.at[m, i, c, d], gr.at[m, i, c, d], device(row, right if d == 0 else left, gcore))

    steps = jnp.where(low, 2 * CHUNKS, CHUNKS)

    def stage(s, hop, drain):
        m, i = s // CHUNKS, s % CHUNKS
        p = jnp.where(m == 0, pmain, row)
        if hop == 0:
            foreign = jnp.logical_and(low, m == 0)

            @pl.when(foreign)
            def _():
                def go(e):
                    c = 2 * x + e

                    @pl.when(needed(p, c, i))
                    def _():
                        if not drain:
                            arrived(wpiece(m, c, i), gr.at[m, i, c, 0])
                        for d in (0, 1):
                            @pl.when(~both(row == 1, x == (nx - 2 if d == 0 else 0)))
                            def _():
                                copy = pass_on(m, c, i, d)
                                copy.wait_send() if drain else copy.start()
                            copy = hand(m, c, i, d)
                            copy.wait_send() if drain else copy.start()
                each(2, go)

            @pl.when(~foreign)
            def _():
                @pl.when(needed(p, col, i))
                def _():
                    for d in (0, 1):
                        for copy in (l_own(m, i, d), hand_own(m, i, d)):
                            copy.wait_send() if drain else copy.start()
                if not drain:
                    other = 2 * x + wcore

                    @pl.when(jnp.logical_and(low, needed(p, other, i)))
                    def _():
                        arrived(wpiece(m, other, i), gr.at[m, i, other, 0])
        else:
            def go(e):
                for d in (0, 1):
                    src = (x + nx - hop) % nx if d == 0 else (x + hop) % nx
                    c = 2 * src + e

                    @pl.when(needed(p, c, i))
                    def _():
                        if not drain:
                            arrived(gpiece(m, c, i, d), gr.at[m, i, c, d])
                        if hop < nx - 1:
                            copy = pass_on(m, c, i, d)
                            copy.wait_send() if drain else copy.start()
                        if hop == 1:
                            @pl.when(both(row == 2, x == nx - 1))
                            def _():
                                ref = gpiece(m, c, i, d)
                                copy = remote(ref, ref, inj.at[i, e, d], gr.at[m, i, c, d], device(1, x, 0))
                                copy.wait_send() if drain else copy.start()
                        copy = hand(m, c, i, d)
                        copy.wait_send() if drain else copy.start()
            each(2, go)

    @pl.when(is_g)
    def _():
        def wave(w):
            @pl.when(both(g0, w == nx - 1))
            def _():
                each(TILES, lambda j: b_again(j).start())
            for hop in reversed(range(nx)):
                s = w - hop

                @pl.when(jnp.logical_and(s >= 0, s < steps))
                def _():
                    stage(s, hop, False)

            done = w - (nx - 1)

            @pl.when(done >= CHUNKS)
            def _():
                extra_rows(done - CHUNKS)
        each(steps + nx - 1, wave)

        def drain(s):
            for hop in range(nx):
                stage(s, hop, True)
        each(steps, drain)

    count = CHUNKS * TILES

    def code_of(t):
        third = t // 3
        tables = [codes(order) for order in ORDERS]
        word = 0
        for n in range(0, len(tables[0]), 3):
            packed = [sum(v * 512**k for k, v in enumerate(table[n:n + 3])) for table in tables]
            at_row = jnp.where(row == 0, packed[0], jnp.where(row == 1, packed[1], packed[2]))
            word = jnp.where(third == n // 3, at_row, word)
        shift = jnp.where(t % 3 == 0, 1, jnp.where(t % 3 == 1, 512, 512 * 512))
        return word // shift % 512

    @pl.when(is_w)
    def _():
        total = jnp.where(low, 2 * count, count)

        def fields(code):
            m = code // EXTRA % 2
            return m, jnp.where(m == 1, row, pmain), code % EXTRA // TILES, code % TILES

        def flag(code, bit):
            return code // bit % 2 == 1

        def fetch(code, slot):
            m, p, i, j = fields(code)

            @pl.when(flag(code, LOAD_B))
            def _():
                for q in range(nrow):
                    @pl.when(q <= p)
                    def _():
                        known = jnp.logical_or(jnp.logical_and(forwards, q == fq), m == 1)

                        @pl.when(both(flag(code, FRESH_B), q != row, ~known))
                        def _():
                            arrived(bg.at[q, :, bcols(j)], br.at[q, j])
                        load_b(q, j, slot)

            @pl.when(flag(code, LOAD_L))
            def _():
                load_l(m, p, i, jnp.logical_or(m == 1, ~low), True)

        def step(t, carry):
            code, slot = carry
            m, p, i, j = fields(code)
            for j2, u2 in enumerate(FORWARD_AT):
                @pl.when(both(row == 1, t == u2))
                def _():
                    forward(j2)

            @pl.when(t == 0)
            def _():
                fetch(code, slot)

            @pl.when(flag(code, LOAD_B))
            def _():
                for q in range(nrow):
                    @pl.when(q <= p)
                    def _():
                        loaded_b(q, slot)

            @pl.when(flag(code, LOAD_L))
            def _():
                loaded_l(m, p, i)

            following = code_of(t + 1)
            other = jnp.where(flag(following, LOAD_B), 1 - slot, slot)

            @pl.when(t + 1 < total)
            def _():
                fetch(following, other)
            n = t % count

            @pl.when(t >= count)
            def _():
                sent(ov.at[n], xs.at[n])
            a, k0 = place(m, i)
            product(a, k0, i, slot, p, n, True)
            home = jnp.logical_and(low, m == 0)

            @pl.when(home)
            def _():
                x_home(n, i, j).start()

            @pl.when(~home)
            def _():
                x_here(n, i, j).start()
            return following, other
        lax.fori_loop(0, total, step, (code_of(0), 0))

    @pl.when(high_g)
    def _():
        arrived(x_ref, xr)

    @pl.when(jnp.logical_or(low, is_w))
    def _():
        each(count, lambda t: sent(ov.at[t], xs.at[t]))

    @pl.when(sends_b)
    def _():
        each(TILES, lambda j: b_first(j).wait_send())

    @pl.when(g0)
    def _():
        each(TILES, lambda j: b_again(j).wait_send())

    @pl.when(forwards)
    def _():
        each(TILES, lambda j: b_forward(j).wait_send())

    def drain(i):
        @pl.when(needed(row, col, i))
        def _():
            @pl.when(~low)
            def _():
                l_to_mirror(i).wait_send()

            @pl.when(is_w)
            def _():
                m = jnp.where(low, 1, 0)
                l_own(m, i, 0).wait_send()
                l_own(m, i, 1).wait_send()

            @pl.when(low_w)
            def _():
                l_to_partner(1, i).wait_send()
    each(CHUNKS, drain)


def solution(mesh):
    nrow, ncol = mesh.shape["row"], mesh.shape["col"]
    spec = P(("batch", "row"), "col")

    def local(l_block, b_block):
        rows, width = l_block.shape
        cols = b_block.shape[1]
        dtype = b_block.dtype
        rc, tw = rows // CHUNKS, cols // TILES
        dma = pltpu.SemaphoreType.DMA
        any_space = pl.BlockSpec(memory_space=pl.ANY)
        out = pl.pallas_call(
            functools.partial(kernel, nrow, ncol // 2),
            out_shape=(
                jax.ShapeDtypeStruct((rows, cols), dtype),
                jax.ShapeDtypeStruct((nrow, rows, cols), dtype),
                jax.ShapeDtypeStruct((2, ncol, rows, width), dtype),
            ),
            in_specs=[any_space] * 2,
            out_specs=(any_space,) * 3,
            scratch_shapes=[
                pltpu.VMEM((CHUNKS + 1, rc, ncol * width), dtype),
                pltpu.VMEM((SLOTS, nrow * rows, tw), dtype),
                pltpu.VMEM((CHUNKS * TILES, rc, tw), dtype),
                pltpu.VMEM((rc, tw), jnp.float32),
                dma((nrow, TILES)),
                dma((TILES,)),
                dma((TILES,)),
                dma((2, CHUNKS, ncol, 2)),
                dma((2, CHUNKS, ncol)),
                dma((2, CHUNKS, ncol, 2)),
                dma((2, CHUNKS, ncol, 2)),
                dma((CHUNKS,)),
                dma((CHUNKS, 2, 2)),
                dma((ncol,)),
                dma((SLOTS, nrow)),
                dma((CHUNKS * TILES,)),
                dma(()),
            ],
            compiler_params=pltpu.CompilerParams(collective_id=0, has_side_effects=True),
        )(l_block, b_block)
        return out[0]

    return jax.shard_map(local, mesh=mesh, in_specs=(spec, spec), out_specs=spec, check_vma=False)
```

profile of v0, /device:TPU:101, one launch (start us, length us, event | category | flops | bytes accessed | tf_op | source)
XLA Modules:
  0.0 322.5 jit_solution(7651828477243533858)
XLA Ops:
  0.0 314.1 %shard_map.28 = (bf16[2048,2048]{1,0:T(8,128)(2,1)}, bf16[4,2048,2048]{2,1,0:T(8,128)(2,1)}, bf16[2,8,2048,1024]{3,2,1,0:T(8,128)(2,1)}) custom-call(bf16[2048,1024]{1,0:T(8,128)(2,1)} %l_ref.1, bf16[2048,2048]{1,0:T(8,128)(2,1)} %b_ref.1), custom_call_target="tpu_custom_call" | custom-call | tf_op jit(solution)/shard_map/pallas_call | solution.py:539
  314.1 8.4 %copy.4 = bf16[2048,2048]{1,0:T(8,128)(2,1)} copy(bf16[2048,2048]{1,0:T(8,128)(2,1)} %get-tuple-element.6) | data formatting | bytes 16777216
where the time goes:
time: 324 us; the launch traced here: 323 us
  Pallas kernels  314 us (97%)
  local copies, waits for them, and re-layouts  8.44 us (3%)
    pallas_call x1, Pallas kernels, local(): pl.pallas_call(functools.partial(kernel, nrow, ncol // 2), out_shape=(jax...  314 us
    unnamed x1, local copies, waits for them, and re-layouts  8.44 us

commit v1 on v0

--- a/solution.py
+++ b/solution.py
@@ -12,18 +12,21 @@
 TILES = 8
 SLOTS = 2
 
+OWN = CHUNKS // 2
+REST = " 24 23 22 21 20 05 15 25 06 16 26 07 17 27 37 36 35 34 33 32 31 30"
 ORDERS = (
-    "00 01 10 11 02 12 03 13 04 14 20 21 22 23 24 05 15 25 06 16 26 30 31 32 33 34 35 36 07 17 27 37",
-    "00 01 10 11 02 12 03 13 20 21 22 23 04 14 24 05 15 25 30 31 32 33 34 35 06 16 26 36 07 17 27 37",
-    "00 01 02 03 10 11 12 13 20 21 22 23 04 14 24 30 31 32 33 34 05 15 25 35 06 16 26 36 07 17 27 37",
+    " ".join(f"E0{j} E1{j}" for j in range(TILES)) + " 00 01 10 11 02 12 03 13 04 14" + REST,
+    " ".join(f"E0{j}" for j in range(TILES)) + " 00 01 10 11 02 12 03 13 "
+    + " ".join(f"E1{j}" for j in range(TILES)) + " 04 14" + REST,
+    " ".join(["E00"] * OWN * TILES) + " 00 01 02 03 10 11 12 13 20 21 22 23 04 14 24 30 31 32 33 34"
+    + " 05 15 25 35 06 16 26 36 07 17 27 37",
 )
-FORWARD_AT = (0, 0, 3, 5, 8, 14, 18, 23)
+FORWARD_AT = (0, 7, 9, 11, 16, 23, 28, 33)
 EXTRA, LOAD_B, FRESH_B, LOAD_L = 32, 64, 128, 256
 
 
 def codes(order):
-    tiles = [(0, int(t[0]), int(t[1])) for t in order.split()]
-    tiles += [(1, i, j) for i in range(CHUNKS) for j in range(TILES)]
+    tiles = [(len(t) - 2, int(t[-2]), int(t[-1])) for t in order.split()]
     out = []
     for n, (extra, i, j) in enumerate(tiles):
         code = i * TILES + j + EXTRA * extra
@@ -137,6 +140,7 @@
     sends_b = ~both(row == 3, core == 0)
     g0 = both(row == 0, core == 0)
     w2 = both(row == 2, core == 0)
+    last2 = both(row == 2, core == 1, x == nx - 1)
 
     def start_b(*js):
         for j in js:
@@ -172,7 +176,7 @@
             forward(j)
         each(TILES, go)
 
-    @pl.when(both(high_g, row == 3))
+    @pl.when(jnp.logical_and(high_g, ~last2))
     def _():
         start_l(0)
         start_l(1)
@@ -182,16 +186,16 @@
         start_l(3)
         start_b(*range(2, TILES))
 
-    @pl.when(both(high_g, row == 2))
-    def _():
-        each(CHUNKS, start_l)
+    @pl.when(low)
+    def _():
         each(TILES, lambda j: b_first(j).start())
 
-    @pl.when(low)
-    def _():
-        each(TILES, lambda j: b_first(j).start())
-
-    def product(a, k0, i, slot, p, t, deep):
+    def place(m, i):
+        return jnp.where(m == 0, i, CHUNKS - 1), jnp.where(m == 0, 0, i * (2 * rows))
+
+    def product(m, i, slot, p, t, deep):
+        a, k0 = place(m, i)
+
         def dot(first, depth):
             lhs = lv[a, :, pl.ds(pl.multiple_of(k0 + first, rows), depth)]
             return jnp.dot(lhs, bv[slot, pl.ds(first, depth), :], preferred_element_type=jnp.float32)
@@ -201,7 +205,7 @@
             def _():
                 acc[...] = dot(0, 2 * rows)
         for odd in (0, 1):
-            for chunk in range(CHUNKS):
+            for chunk in range(CHUNKS if deep else OWN):
                 depth = odd * rows + (chunk + 1) * rc
 
                 @pl.when(both(p % 2 == odd, i == chunk))
@@ -212,14 +216,11 @@
                     else:
                         ov[t] = dot(0, depth).astype(ov.dtype)
 
-    def place(m, i):
-        return jnp.where(m == 0, i, CHUNKS), jnp.where(m == 0, 0, i % 2 * (2 * rows))
-
     def copy_l(m, i, c, local):
         a, k0 = place(m, i)
         src = l_ref.at[lrows(i), :] if local else wpiece(m, c, i)
         to = lv.at[a, :, pl.ds(pl.multiple_of(k0 + c * width, width), width)]
-        return pltpu.make_async_copy(src, to, lvs.at[c])
+        return pltpu.make_async_copy(src, to, lvs.at[i, c])
 
     def load_l(m, p, i, own, wait):
         def start(c):
@@ -269,8 +270,6 @@
         return pltpu.make_async_copy(ov.at[t], x_ref.at[lrows(i), bcols(j)], xs.at[t])
 
     def extra_rows(i):
-        a, k0 = place(1, i)
-
         def start(j):
             for q in (0, 1):
                 @pl.when(q <= row)
@@ -293,7 +292,7 @@
             @pl.when(j < TILES - 1)
             def _():
                 start(j + 1)
-            product(a, k0, i, j % SLOTS, row, i * TILES + j, False)
+            product(1, i, j % SLOTS, row, i * TILES + j, False)
             x_here(i * TILES + j, i, j).start()
         each(TILES, tile)
 
@@ -311,7 +310,7 @@
     steps = jnp.where(low, 2 * CHUNKS, CHUNKS)
 
     def stage(s, hop, drain):
-        m, i = s // CHUNKS, s % CHUNKS
+        m, i = jnp.where(low, s % 2, 0), jnp.where(low, s // 2, s)
         p = jnp.where(m == 0, pmain, row)
         if hop == 0:
             foreign = jnp.logical_and(low, m == 0)
@@ -373,21 +372,33 @@
     @pl.when(is_g)
     def _():
         def wave(w):
-            @pl.when(both(g0, w == nx - 1))
+            @pl.when(both(g0, w == nx + 2))
             def _():
                 each(TILES, lambda j: b_again(j).start())
+            @pl.when(w == 0)
+            def _():
+                @pl.when(low)
+                def _():
+                    each(OWN, lambda i: stage(2 * i + 1, 0, False))
+
+                @pl.when(~low)
+                def _():
+                    each(steps, lambda s: stage(s, 0, False))
             for hop in reversed(range(nx)):
                 s = w - hop
 
-                @pl.when(jnp.logical_and(s >= 0, s < steps))
+                @pl.when(both(s >= 0, s < steps, True if hop else both(low, s != 1, s != 3)))
                 def _():
                     stage(s, hop, False)
 
-            done = w - (nx - 1)
-
-            @pl.when(done >= CHUNKS)
-            def _():
-                extra_rows(done - CHUNKS)
+            for at, first, n in ((0, 0, 1), (1, 1, 2), (nx, 3, TILES - 3)):
+                @pl.when(both(last2, w == at))
+                def _():
+                    each(n, lambda k: b_first(first + k).start())
+
+            @pl.when(jnp.logical_and(low, w >= steps + nx - 1 - OWN))
+            def _():
+                extra_rows(w - (steps + nx - 1 - OWN))
         each(steps + nx - 1, wave)
 
         def drain(s):
@@ -410,8 +421,6 @@
 
     @pl.when(is_w)
     def _():
-        total = jnp.where(low, 2 * count, count)
-
         def fields(code):
             m = code // EXTRA % 2
             return m, jnp.where(m == 1, row, pmain), code % EXTRA // TILES, code % TILES
@@ -427,7 +436,7 @@
                 for q in range(nrow):
                     @pl.when(q <= p)
                     def _():
-                        known = jnp.logical_or(jnp.logical_and(forwards, q == fq), m == 1)
+                        known = jnp.logical_or(jnp.logical_and(forwards, q == fq), both(low, m == 0, q <= row))
 
                         @pl.when(both(flag(code, FRESH_B), q != row, ~known))
                         def _():
@@ -437,6 +446,9 @@
             @pl.when(flag(code, LOAD_L))
             def _():
                 load_l(m, p, i, jnp.logical_or(m == 1, ~low), True)
+
+        first = jnp.where(low, 0, OWN * TILES)
+        total = OWN * TILES + count
 
         def step(t, carry):
             code, slot = carry
@@ -446,7 +458,7 @@
                 def _():
                     forward(j2)
 
-            @pl.when(t == 0)
+            @pl.when(t == first)
             def _():
                 fetch(code, slot)
 
@@ -468,13 +480,12 @@
             def _():
                 fetch(following, other)
             n = t % count
-
-            @pl.when(t >= count)
+            home = jnp.logical_and(low, m == 0)
+
+            @pl.when(jnp.logical_and(low, t >= count))
             def _():
                 sent(ov.at[n], xs.at[n])
-            a, k0 = place(m, i)
-            product(a, k0, i, slot, p, n, True)
-            home = jnp.logical_and(low, m == 0)
+            product(m, i, slot, p, n, True)
 
             @pl.when(home)
             def _():
@@ -484,15 +495,29 @@
             def _():
                 x_here(n, i, j).start()
             return following, other
-        lax.fori_loop(0, total, step, (code_of(0), 0))
+        lax.fori_loop(first, total, step, (code_of(first), 0))
 
     @pl.when(high_g)
     def _():
         arrived(x_ref, xr)
 
-    @pl.when(jnp.logical_or(low, is_w))
+    @pl.when(is_w)
     def _():
         each(count, lambda t: sent(ov.at[t], xs.at[t]))
+
+    @pl.when(low_g)
+    def _():
+        each(OWN * TILES, lambda t: sent(ov.at[t], xs.at[t]))
+
+    @pl.when(low_w)
+    def _():
+        def piece(n):
+            c, i = n // OWN, OWN + n % OWN
+
+            @pl.when(jnp.logical_and(needed(row, c, i), c != col))
+            def _():
+                arrived(wpiece(1, c, i), wr.at[1, i, c])
+        each(2 * nx * OWN, piece)
 
     @pl.when(sends_b)
     def _():
@@ -523,6 +548,107 @@
             def _():
                 l_to_partner(1, i).wait_send()
     each(CHUNKS, drain)
+
+
+def finish(nx, l_ref, b_ref, part, bg, lb, x_ref, lv, bv, ov, lvs, bvs, xs):
+    rows, width = l_ref.shape
+    rc, tw = rows // CHUNKS, b_ref.shape[1] // TILES
+    row, col = lax.axis_index("row"), lax.axis_index("col")
+    low = row < 2
+
+    def each(n, body):
+        lax.fori_loop(0, n, lambda k, carry: (body(k), carry)[1], 0)
+
+    def lrows(i):
+        return pl.ds(pl.multiple_of(i * rc, rc), rc)
+
+    def bcols(j):
+        return pl.ds(pl.multiple_of(j * tw, tw), tw)
+
+    def needed(c, i):
+        return jnp.logical_or(c <= 2 * row, jnp.logical_and(c == 2 * row + 1, i >= CHUNKS // 2))
+
+    def copy_l(i, c, local):
+        src = l_ref.at[lrows(i), :] if local else lb.at[1, c, lrows(i), :]
+        return pltpu.make_async_copy(src, lv.at[i, :, pl.ds(c * width, width)], lvs.at[i, c])
+
+    def copy_b(j, q, local):
+        src = b_ref.at[:, bcols(j)] if local else bg.at[q, :, bcols(j)]
+        return pltpu.make_async_copy(src, bv.at[j % SLOTS, pl.ds(q * rows, rows), :], bvs.at[j % SLOTS, q])
+
+    def load_b(j):
+        for q in (0, 1):
+            @pl.when(q == row)
+            def _():
+                copy_b(j, q, True).start()
+
+            @pl.when(q < row)
+            def _():
+                copy_b(j, q, False).start()
+
+    def write(i, j):
+        return pltpu.make_async_copy(ov.at[i * TILES + j], x_ref.at[lrows(i), bcols(j)], xs.at[i * TILES + j])
+
+    def read(n):
+        return pltpu.make_async_copy(part.at[lrows(n // TILES), bcols(n % TILES)], ov.at[n], xs.at[n])
+
+    def turn(n):
+        read(n).wait()
+        write(n // TILES, n % TILES).start()
+
+    @pl.when(low)
+    def _():
+        load_b(0)
+
+        def load_l(i):
+            for c in range(4):
+                @pl.when(jnp.logical_and(needed(c, i), c == col))
+                def _():
+                    copy_l(i, c, True).start()
+
+                @pl.when(jnp.logical_and(needed(c, i), c != col))
+                def _():
+                    copy_l(i, c, False).start()
+        each(OWN, lambda i: load_l(OWN + i))
+        each(OWN * TILES, lambda n: read(n).start())
+
+        def tile(n):
+            i, j = OWN + n % OWN, n // OWN
+
+            @pl.when(i == OWN)
+            def _():
+                for q in (0, 1):
+                    @pl.when(q <= row)
+                    def _():
+                        copy_b(j, q, True).wait()
+
+                @pl.when(j < TILES - 1)
+                def _():
+                    load_b(j + 1)
+
+            @pl.when(j == 0)
+            def _():
+                for c in range(4):
+                    @pl.when(needed(c, i))
+                    def _():
+                        copy_l(i, c, True).wait()
+            for p in (0, 1):
+                for chunk in range(OWN, CHUNKS):
+                    depth = p * rows + (chunk + 1) * rc
+
+                    @pl.when(jnp.logical_and(row == p, i == chunk))
+                    def _():
+                        ov[i * TILES + j] = jnp.dot(
+                            lv[i, :, :depth], bv[j % SLOTS, :depth, :], preferred_element_type=jnp.float32
+                        ).astype(ov.dtype)
+            write(i, j).start()
+        each(OWN * TILES, tile)
+
+    @pl.when(~low)
+    def _():
+        each(CHUNKS * TILES, lambda n: read(n).start())
+    each(jnp.where(low, OWN, CHUNKS) * TILES, turn)
+    each(CHUNKS * TILES, lambda n: write(n // TILES, n % TILES).wait())
 
 
 def solution(mesh):
@@ -536,7 +662,7 @@
         rc, tw = rows // CHUNKS, cols // TILES
         dma = pltpu.SemaphoreType.DMA
         any_space = pl.BlockSpec(memory_space=pl.ANY)
-        out = pl.pallas_call(
+        part, blocks, strips = pl.pallas_call(
             functools.partial(kernel, nrow, ncol // 2),
             out_shape=(
                 jax.ShapeDtypeStruct((rows, cols), dtype),
@@ -546,7 +672,7 @@
             in_specs=[any_space] * 2,
             out_specs=(any_space,) * 3,
             scratch_shapes=[
-                pltpu.VMEM((CHUNKS + 1, rc, ncol * width), dtype),
+                pltpu.VMEM((CHUNKS, rc, ncol * width), dtype),
                 pltpu.VMEM((SLOTS, nrow * rows, tw), dtype),
                 pltpu.VMEM((CHUNKS * TILES, rc, tw), dtype),
                 pltpu.VMEM((rc, tw), jnp.float32),
@@ -559,13 +685,26 @@
                 dma((2, CHUNKS, ncol, 2)),
                 dma((CHUNKS,)),
                 dma((CHUNKS, 2, 2)),
-                dma((ncol,)),
+                dma((CHUNKS, ncol)),
                 dma((SLOTS, nrow)),
                 dma((CHUNKS * TILES,)),
                 dma(()),
             ],
             compiler_params=pltpu.CompilerParams(collective_id=0, has_side_effects=True),
         )(l_block, b_block)
-        return out[0]
+        return pl.pallas_call(
+            functools.partial(finish, ncol // 2),
+            out_shape=jax.ShapeDtypeStruct((rows, cols), dtype),
+            in_specs=[any_space] * 5,
+            out_specs=any_space,
+            scratch_shapes=[
+                pltpu.VMEM((CHUNKS, rc, 4 * width), dtype),
+                pltpu.VMEM((SLOTS, 2 * rows, tw), dtype),
+                pltpu.VMEM((CHUNKS * TILES, rc, tw), dtype),
+                dma((CHUNKS, 4)),
+                dma((SLOTS, 2)),
+                dma((CHUNKS * TILES,)),
+            ],
+        )(l_block, b_block, part, blocks, strips)
 
     return jax.shard_map(local, mesh=mesh, in_specs=(spec, spec), out_specs=spec, check_vma=False)

time: 324 us -> 268 us (0.83)
  the two profiles are of different devices: /device:TPU:101 before, /device:TPU:97 now
where the time goes in v1:
time: 268 us; the launch traced here: 264 us
  Pallas kernels  263 us (98%)
    pallas_call x1, Pallas kernels, local(): pl.pallas_call(functools.partial(kernel, nrow, ncol // 2), out_shape=(jax...  246 us
    pallas_call x1, Pallas kernels, local(): pl.pallas_call(functools.partial(finish, ncol // 2), out_shape=jax.ShapeD...  17.1 us

profile of v1, /device:TPU:97, one launch (start us, length us, event | category | flops | bytes accessed | tf_op | source)
XLA Modules:
  0.0 263.6 jit_solution(12766922411052182348)
XLA Ops:
  0.0 246.3 %shard_map.28 = (bf16[2048,2048]{1,0:T(8,128)(2,1)}, bf16[4,2048,2048]{2,1,0:T(8,128)(2,1)}, bf16[2,8,2048,1024]{3,2,1,0:T(8,128)(2,1)}) custom-call(bf16[2048,1024]{1,0:T(8,128)(2,1)} %l_ref.3, bf16[2048,2048]{1,0:T(8,128)(2,1)} %b_ref.3), custom_call_target="tpu_custom_call" | custom-call | tf_op jit(solution)/shard_map/pallas_call | solution.py:665
  246.4 17.1 %shard_map.29 = bf16[2048,2048]{1,0:T(8,128)(2,1)} custom-call(bf16[2048,1024]{1,0:T(8,128)(2,1)} %l_ref.3, bf16[2048,2048]{1,0:T(8,128)(2,1)} %b_ref.3, bf16[2048,2048]{1,0:T(8,128)(2,1)} %get-tuple-element.8.part, bf16[4,2048,2048]{2,1,0:T(8,128)(2,1)} %get-tuple-element.9.bg, bf16[2,8,2048,1024]{3,2,1,0:T(8,128)(2,1)} %get-tuple-element.10.lb), custom_call_target="tpu_custom_call" | custom-call | tf_op jit(solution)/shard_map/pallas_call | solution.py:695

commit v2 on v1

--- a/solution.py
+++ b/solution.py
@@ -15,13 +15,14 @@
 OWN = CHUNKS // 2
 REST = " 24 23 22 21 20 05 15 25 06 16 26 07 17 27 37 36 35 34 33 32 31 30"
 ORDERS = (
-    " ".join(f"E0{j} E1{j}" for j in range(TILES)) + " 00 01 10 11 02 12 03 13 04 14" + REST,
-    " ".join(f"E0{j}" for j in range(TILES)) + " 00 01 10 11 02 12 03 13 "
-    + " ".join(f"E1{j}" for j in range(TILES)) + " 04 14" + REST,
-    " ".join(["E00"] * OWN * TILES) + " 00 01 02 03 10 11 12 13 20 21 22 23 04 14 24 30 31 32 33 34"
-    + " 05 15 25 35 06 16 26 36 07 17 27 37",
+    " ".join(f"E{i}{j}" for j in range(TILES) for i in range(CHUNKS)) + " 00 01 02 10 11 12 03 13 04 14" + REST,
+    " ".join(f"E0{j}" for j in range(TILES)) + " 00 01 10 11 02 12 "
+    + " ".join(f"E1{j}" for j in range(TILES))
+    + " 03 13 23 22 21 20 04 14 24 05 15 25 06 16 26 07 17 27 37 36 35 34 33 32 31 30",
+    "00 01 02 03 10 11 12 13 20 21 22 23 04 14 24 30 31 32 33 34 05 15 25 35 06 16 26 36 07 17 27 37",
 )
-FORWARD_AT = (0, 7, 9, 11, 16, 23, 28, 33)
+SPAN = 2 * CHUNKS * TILES
+FORWARD_AT = (16, 20, 27, 37, 43, 46, 49, 52)
 EXTRA, LOAD_B, FRESH_B, LOAD_L = 32, 64, 128, 256
 
 
@@ -37,7 +38,7 @@
         if (extra, i) not in [(e, a) for e, a, _ in tiles[:n]]:
             code += LOAD_L
         out.append(code)
-    return out
+    return [0] * (SPAN - len(out)) + out
 
 
 def kernel(nrow, nx, l_ref, b_ref, x_ref, bg, lb, lv, bv, ov, acc,
@@ -167,31 +168,42 @@
 
     @pl.when(high_w)
     def _():
-        each(CHUNKS, start_l)
+        each(jnp.where(w2, OWN, CHUNKS), start_l)
 
         def go(j):
             @pl.when(w2)
             def _():
                 b_first(j).start()
             forward(j)
+            for j2, i in ((4, 2), (7, 3)):
+                @pl.when(jnp.logical_and(w2, j == j2))
+                def _():
+                    start_l(i)
         each(TILES, go)
 
-    @pl.when(jnp.logical_and(high_g, ~last2))
+    @pl.when(both(high_g, row == 3))
+    def _():
+        each(CHUNKS, start_l)
+        each(TILES, lambda j: b_first(j).start())
+
+    @pl.when(both(high_g, row == 2, ~last2))
     def _():
         start_l(0)
         start_l(1)
-        start_b(0)
+        start_b(0, 1)
         start_l(2)
-        start_b(1)
+        start_b(2)
         start_l(3)
-        start_b(*range(2, TILES))
+        start_b(*range(3, TILES))
 
     @pl.when(low)
     def _():
         each(TILES, lambda j: b_first(j).start())
 
     def place(m, i):
-        return jnp.where(m == 0, i, CHUNKS - 1), jnp.where(m == 0, 0, i * (2 * rows))
+        own_a = jnp.where(row == 0, CHUNKS - 1 - i // 2, CHUNKS - 1)
+        own_k = i % 2 * (2 * rows)
+        return jnp.where(m == 0, i, own_a), jnp.where(m == 0, 0, own_k)
 
     def product(m, i, slot, p, t, deep):
         a, k0 = place(m, i)
@@ -205,7 +217,7 @@
             def _():
                 acc[...] = dot(0, 2 * rows)
         for odd in (0, 1):
-            for chunk in range(CHUNKS if deep else OWN):
+            for chunk in range(CHUNKS):
                 depth = odd * rows + (chunk + 1) * rc
 
                 @pl.when(both(p % 2 == odd, i == chunk))
@@ -269,6 +281,16 @@
     def x_here(t, i, j):
         return pltpu.make_async_copy(ov.at[t], x_ref.at[lrows(i), bcols(j)], xs.at[t])
 
+    def extra_columns(j):
+        slot = j % SLOTS
+        load_b(0, j, slot)
+        loaded_b(0, slot)
+
+        def tile(i):
+            product(1, i, slot, row, i * TILES + j, False)
+            x_here(i * TILES + j, i, j).start()
+        each(CHUNKS, tile)
+
     def extra_rows(i):
         def start(j):
             for q in (0, 1):
@@ -310,7 +332,8 @@
     steps = jnp.where(low, 2 * CHUNKS, CHUNKS)
 
     def stage(s, hop, drain):
-        m, i = jnp.where(low, s % 2, 0), jnp.where(low, s // 2, s)
+        m = jnp.where(row == 0, 1 - s // CHUNKS, jnp.where(row == 1, s % 2, 0))
+        i = jnp.where(row == 1, s // 2, s % CHUNKS)
         p = jnp.where(m == 0, pmain, row)
         if hop == 0:
             foreign = jnp.logical_and(low, m == 0)
@@ -372,22 +395,22 @@
     @pl.when(is_g)
     def _():
         def wave(w):
-            @pl.when(both(g0, w == nx + 2))
+            @pl.when(both(g0, w == nx + 3))
             def _():
                 each(TILES, lambda j: b_again(j).start())
             @pl.when(w == 0)
             def _():
-                @pl.when(low)
+                @pl.when(row == 1)
                 def _():
                     each(OWN, lambda i: stage(2 * i + 1, 0, False))
 
-                @pl.when(~low)
-                def _():
-                    each(steps, lambda s: stage(s, 0, False))
+                @pl.when(row != 1)
+                def _():
+                    each(CHUNKS, lambda s: stage(s, 0, False))
             for hop in reversed(range(nx)):
                 s = w - hop
 
-                @pl.when(both(s >= 0, s < steps, True if hop else both(low, s != 1, s != 3)))
+                @pl.when(both(s >= 0, s < steps, True if hop else jnp.where(row == 1, both(s != 1, s != 3), s >= CHUNKS)))
                 def _():
                     stage(s, hop, False)
 
@@ -396,10 +419,18 @@
                 def _():
                     each(n, lambda k: b_first(first + k).start())
 
-            @pl.when(jnp.logical_and(low, w >= steps + nx - 1 - OWN))
-            def _():
-                extra_rows(w - (steps + nx - 1 - OWN))
+            k = w - (steps + nx - 4)
+
+            @pl.when(both(row == 1, k >= 0, k < OWN))
+            def _():
+                extra_rows(k)
         each(steps + nx - 1, wave)
+
+        @pl.when(row == 0)
+        def _():
+            each(CHUNKS, lambda i: load_l(1, row, i, True, False))
+            each(CHUNKS, lambda i: loaded_l(1, row, i))
+            each(TILES, extra_columns)
 
         def drain(s):
             for hop in range(nx):
@@ -447,8 +478,7 @@
             def _():
                 load_l(m, p, i, jnp.logical_or(m == 1, ~low), True)
 
-        first = jnp.where(low, 0, OWN * TILES)
-        total = OWN * TILES + count
+        first = jnp.where(row == 0, 0, jnp.where(row == 1, OWN * TILES, count))
 
         def step(t, carry):
             code, slot = carry
@@ -476,13 +506,13 @@
             following = code_of(t + 1)
             other = jnp.where(flag(following, LOAD_B), 1 - slot, slot)
 
-            @pl.when(t + 1 < total)
+            @pl.when(t + 1 < SPAN)
             def _():
                 fetch(following, other)
             n = t % count
             home = jnp.logical_and(low, m == 0)
 
-            @pl.when(jnp.logical_and(low, t >= count))
+            @pl.when(t >= first + count)
             def _():
                 sent(ov.at[n], xs.at[n])
             product(m, i, slot, p, n, True)
@@ -495,7 +525,7 @@
             def _():
                 x_here(n, i, j).start()
             return following, other
-        lax.fori_loop(first, total, step, (code_of(first), 0))
+        lax.fori_loop(first, SPAN, step, (code_of(first), 0))
 
     @pl.when(high_g)
     def _():
@@ -507,9 +537,9 @@
 
     @pl.when(low_g)
     def _():
-        each(OWN * TILES, lambda t: sent(ov.at[t], xs.at[t]))
-
-    @pl.when(low_w)
+        each(jnp.where(row == 0, CHUNKS, OWN) * TILES, lambda t: sent(ov.at[t], xs.at[t]))
+
+    @pl.when(jnp.logical_and(low_w, row == 1))
     def _():
         def piece(n):
             c, i = n // OWN, OWN + n % OWN
@@ -554,7 +584,9 @@
     rows, width = l_ref.shape
     rc, tw = rows // CHUNKS, b_ref.shape[1] // TILES
     row, col = lax.axis_index("row"), lax.axis_index("col")
-    low = row < 2
+    low = row == 1
+    done = jnp.where(low, OWN, CHUNKS)
+    left = CHUNKS - done
 
     def each(n, body):
         lax.fori_loop(0, n, lambda k, carry: (body(k), carry)[1], 0)
@@ -609,13 +641,13 @@
                 @pl.when(jnp.logical_and(needed(c, i), c != col))
                 def _():
                     copy_l(i, c, False).start()
-        each(OWN, lambda i: load_l(OWN + i))
-        each(OWN * TILES, lambda n: read(n).start())
+        each(left, lambda i: load_l(done + i))
+        each(done * TILES, lambda n: read(n).start())
 
         def tile(n):
-            i, j = OWN + n % OWN, n // OWN
-
-            @pl.when(i == OWN)
+            i, j = done + n % left, n // left
+
+            @pl.when(i == done)
             def _():
                 for q in (0, 1):
                     @pl.when(q <= row)
@@ -632,22 +664,21 @@
                     @pl.when(needed(c, i))
                     def _():
                         copy_l(i, c, True).wait()
-            for p in (0, 1):
-                for chunk in range(OWN, CHUNKS):
-                    depth = p * rows + (chunk + 1) * rc
-
-                    @pl.when(jnp.logical_and(row == p, i == chunk))
-                    def _():
-                        ov[i * TILES + j] = jnp.dot(
-                            lv[i, :, :depth], bv[j % SLOTS, :depth, :], preferred_element_type=jnp.float32
-                        ).astype(ov.dtype)
+            for chunk in range(OWN, CHUNKS):
+                depth = rows + (chunk + 1) * rc
+
+                @pl.when(i == chunk)
+                def _():
+                    ov[i * TILES + j] = jnp.dot(
+                        lv[i, :, :depth], bv[j % SLOTS, :depth, :], preferred_element_type=jnp.float32
+                    ).astype(ov.dtype)
             write(i, j).start()
-        each(OWN * TILES, tile)
+        each(left * TILES, tile)
 
     @pl.when(~low)
     def _():
         each(CHUNKS * TILES, lambda n: read(n).start())
-    each(jnp.where(low, OWN, CHUNKS) * TILES, turn)
+    each(done * TILES, turn)
     each(CHUNKS * TILES, lambda n: write(n // TILES, n % TILES).wait())
 
 

time: 268 us -> 263 us (0.981)
  the two profiles are of different devices: /device:TPU:97 before, /device:TPU:103 now
where the time goes in v2:
time: 263 us; the launch traced here: 262 us
  Pallas kernels  262 us (100%)
    pallas_call x1, Pallas kernels, local(): pl.pallas_call(functools.partial(kernel, nrow, ncol // 2), out_shape=(jax...  255 us
    pallas_call x1, Pallas kernels, local(): pl.pallas_call(functools.partial(finish, ncol // 2), out_shape=jax.ShapeD...  7.28 us

profile of v2, /device:TPU:103, one launch (start us, length us, event | category | flops | bytes accessed | tf_op | source)
XLA Modules:
  0.0 262.2 jit_solution(3583743259445646320)
XLA Ops:
  0.0 254.8 %shard_map.28 = (bf16[2048,2048]{1,0:T(8,128)(2,1)}, bf16[4,2048,2048]{2,1,0:T(8,128)(2,1)}, bf16[2,8,2048,1024]{3,2,1,0:T(8,128)(2,1)}) custom-call(bf16[2048,1024]{1,0:T(8,128)(2,1)} %l_ref.3, bf16[2048,2048]{1,0:T(8,128)(2,1)} %b_ref.3), custom_call_target="tpu_custom_call" | custom-call | tf_op jit(solution)/shard_map/pallas_call | solution.py:696
  254.8 7.3 %shard_map.29 = bf16[2048,2048]{1,0:T(8,128)(2,1)} custom-call(bf16[2048,1024]{1,0:T(8,128)(2,1)} %l_ref.3, bf16[2048,2048]{1,0:T(8,128)(2,1)} %b_ref.3, bf16[2048,2048]{1,0:T(8,128)(2,1)} %get-tuple-element.8.part, bf16[4,2048,2048]{2,1,0:T(8,128)(2,1)} %get-tuple-element.9.bg, bf16[2,8,2048,1024]{3,2,1,0:T(8,128)(2,1)} %get-tuple-element.10.lb), custom_call_target="tpu_custom_call" | custom-call | tf_op jit(solution)/shard_map/pallas_call | solution.py:726
